TPU v7x, 512 devices: a whole 4x4x16 slice. The times are simulated.
512 devices in a mesh: client: 4 (over z_hi), expert: 16 (over y, x), shard: 8 (over z_lo, core).
Axes of the slice: x: 4, y: 4, z: 16 (z_hi: 4, z_lo: 4; z = z_hi * 4 + z_lo), core: 2. Of those that a mesh axis runs over, the one named last changes fastest.
Arguments:
- tokens: bfloat16 [4, 2048, 2048], P('client', 'expert'), may hold values from -6 to 6
- target: bfloat16 [4, 2048, 2048], P('client', 'expert'), may hold values from -6 to 6
- routes: int32 [4, 2048, 2], P('client', 'expert'), may hold values from 0 to 7, all different within a row; in each aligned block of 128 rows (0 to 127, 128 to 255, ..., all dimensions but the last counted through in order) at most 32 rows name the same one
- gate_weights: float32 [4, 2048, 2], P('client', 'expert'), may hold values from 0.1 to 1
- counts: int32 [4], replicated, may hold values from 512 to 2048
- gate_proj: bfloat16 [57344, 2048], P(('expert', 'shard'), 'client'), may hold values from -0.125 to 0.125
- up_proj: bfloat16 [57344, 2048], P(('expert', 'shard'), 'client'), may hold values from -0.125 to 0.125
- down_proj: bfloat16 [57344, 2048], P(('expert', 'shard'), 'client'), may hold values from -0.0625 to 0.0625
- correction: bfloat16 [4, 57344, 2048], P('client', ('expert', 'shard')), may hold values from -6 to 6
Outputs:
- pseudo_gradient: float32 [57344, 2048], P(('expert', 'shard'), 'client')
Inputs may be any that keep to these rules, and one draw needn't show every extreme that they name: `routes`: in each aligned block of 128 rows of a client, every expert is named by exactly 32 rows; the 2 ids of a row differ.
All inputs are finite; a program needn't handle non-finite values.
Results may differ from a plain program's by a relative error of at most 0.015.
Values may be sent and summed in bfloat16 or wider, within the bound.
No kernel may reach another device: no remote copies, remote signals or barrier semaphores. Data moves between devices by JAX's collectives and lax.ppermute only.
A program may use at most 64 MiB of HBM per device.

v0:
```python
import jax
import jax.numpy as jnp
from jax import lax
from jax.sharding import PartitionSpec as P

FF = 7168
EXPERTS = 8
LOCAL_STEPS = 2


def sent_together(arrays, axis, dim, along):
    ends, at = ([], 0)
    for a in arrays[:-1]:
        at += a.shape[along]
        ends.append(at)
    both = jnp.concatenate(arrays, axis=along)
    return tuple(jnp.split(lax.all_gather(both, axis, axis=dim, tiled=True), ends, axis=along))


def in_blocks(x, dim, peers):
    shape = x.shape
    parts = x.reshape(*shape[:dim], peers, shape[dim] // peers, *shape[dim + 1 :])
    return jnp.moveaxis(parts, dim, 0)


def sum_at_owner(x, axis, dim):
    peers = lax.axis_size(axis)
    parts = lax.all_to_all(in_blocks(x, dim, peers), axis, 0, 0, tiled=True)
    return jnp.sum(parts.astype(jnp.float32), axis=0)


def local(tokens, target, routes, gate_weights, counts, gate_proj, up_proj, down_proj, correction):
    expert_count = lax.axis_size("expert")
    shard_count = lax.axis_size("shard")
    client_count = lax.axis_size("client")
    expert_index = lax.axis_index("expert")
    shard_index = lax.axis_index("shard")
    client_index = lax.axis_index("client")
    unit_count = down_proj.shape[0]
    token_count = tokens.shape[1]
    top_count = routes.shape[2]
    feature_width = tokens.shape[2]
    capacity = token_count * top_count // EXPERTS
    per_index = shard_count * unit_count
    hosted = max(1, per_index // FF)
    copies = max(1, FF // per_index)
    own_expert = (expert_index * shard_count + shard_index) * unit_count // FF
    first_expert = expert_index * per_index // FF
    share_width = feature_width // shard_count
    flat_routes = routes[0].reshape(-1)
    onehot = (flat_routes[:, None] == jnp.arange(EXPERTS, dtype=jnp.int32)[None, :]).astype(
        jnp.int32
    )
    rank_of = jnp.sum((jnp.cumsum(onehot, axis=0) - 1) * onehot, axis=1)
    slot_of = flat_routes * capacity + rank_of
    source_of = (
        jnp.zeros((EXPERTS * capacity,), jnp.int32)
        .at[slot_of]
        .set(jnp.arange(token_count * top_count, dtype=jnp.int32))
    )

    def arrange(slots, width):
        blocks = slots.reshape(EXPERTS, capacity, width)
        return jnp.repeat(blocks, copies, axis=0)

    def own_of(arrived):
        return arrived.reshape(expert_count * capacity, feature_width)

    token_slots = jnp.take(tokens[0], source_of // top_count, axis=0)
    send_blocks = arrange(token_slots, feature_width)
    send_arrived = lax.all_to_all(send_blocks, "expert", split_axis=0, concat_axis=0, tiled=True)
    features = own_of(send_arrived)
    contract = (((1,), (1,)), ((), ()))
    full_gate, full_up = sent_together((gate_proj, up_proj), "client", 1, 0)
    gate_pre = lax.dot_general(features, full_gate, contract, preferred_element_type=jnp.float32)
    up_pre = lax.dot_general(features, full_up, contract, preferred_element_type=jnp.float32)
    hidden = (jax.nn.silu(gate_pre) * up_pre).astype(jnp.bfloat16)
    down_full = lax.all_gather(down_proj, "client", axis=1, tiled=True)
    control = correction[0]
    grad_sum = None
    gate_rows = gate_weights[0]
    positions = expert_index * token_count + jnp.arange(token_count, dtype=jnp.int32)
    live_rows = (positions < counts[client_index]).astype(jnp.float32)
    sender_group = (
        (jnp.arange(expert_count, dtype=jnp.int32) * per_index // FF)[:, None]
        + jnp.arange(hosted, dtype=jnp.int32)[None, :]
    ).reshape(-1)
    group_pick = (jnp.arange(EXPERTS, dtype=jnp.int32)[:, None] == sender_group[None, :]).astype(
        jnp.float32
    )
    hosted_mask = (jnp.arange(hosted, dtype=jnp.int32) == own_expert - first_expert).astype(
        jnp.float32
    )
    target_rows = target[0].astype(jnp.float32)
    step_size = 2.0 / FF
    for step_number in range(LOCAL_STEPS):
        if step_number == 0:
            current = down_full
        else:
            current = (
                down_full.astype(jnp.float32)
                - step_size * (grad_sum + float(step_number) * control.astype(jnp.float32))
            ).astype(jnp.bfloat16)
        partial_value = jnp.dot(hidden, current, preferred_element_type=jnp.float32).astype(
            jnp.bfloat16
        )
        placed = (
            partial_value.astype(jnp.float32).reshape(expert_count, 1, capacity, feature_width)
            * hosted_mask[None, :, None, None]
        )
        placed = placed.reshape(expert_count, hosted * capacity, feature_width)
        shared = sum_at_owner(placed.astype(jnp.bfloat16), "shard", 2)
        returned = lax.all_to_all(
            shared.astype(jnp.bfloat16), "expert", split_axis=0, concat_axis=0, tiled=True
        ).astype(shared.dtype)
        slot_sums = jnp.einsum("ej,jcd->ecd", group_pick, returned, precision=lax.Precision.HIGHEST)
        slot_sums = slot_sums.reshape(EXPERTS * capacity, share_width)
        picked = jnp.take(slot_sums, slot_of, axis=0).reshape(token_count, top_count, share_width)
        output = jnp.sum(gate_rows[:, :, None] * picked, axis=1)
        target_share = lax.dynamic_slice_in_dim(
            target_rows, shard_index * share_width, share_width, 1
        )
        residual = live_rows[:, None] * (output - target_share)
        cotangent = (gate_rows[:, :, None] * residual[:, None, :]).astype(jnp.bfloat16)
        cotangent = cotangent.reshape(token_count * top_count, share_width)
        blocks = arrange(jnp.take(cotangent, source_of, axis=0), share_width)
        arrived = lax.all_to_all(blocks, "expert", split_axis=0, concat_axis=0, tiled=True)
        arrived = own_of(lax.all_gather(arrived, "shard", axis=2, tiled=True))
        gradient = lax.dot_general(
            hidden, arrived, (((0,), (0,)), ((), ())), preferred_element_type=jnp.float32
        )
        if step_number == 0:
            grad_sum = gradient
        else:
            grad_sum = grad_sum + gradient
    weight_share = counts[client_index].astype(jnp.float32) / jnp.sum(counts).astype(jnp.float32)
    client_term = (weight_share * (grad_sum / LOCAL_STEPS + control.astype(jnp.float32))).astype(
        jnp.bfloat16
    )
    client_term = client_term.reshape(unit_count, client_count, feature_width // client_count)
    received = lax.all_to_all(client_term, "client", split_axis=1, concat_axis=1, tiled=True)
    return jnp.sum(received.astype(jnp.float32), axis=1)


def solution(mesh):
    return jax.shard_map(
        local,
        mesh=mesh,
        in_specs=(
            P("client", "expert", None),
            P("client", "expert", None),
            P("client", "expert", None),
            P("client", "expert", None),
            P(),
            P(("expert", "shard"), "client"),
            P(("expert", "shard"), "client"),
            P(("expert", "shard"), "client"),
            P("client", ("expert", "shard"), None),
        ),
        out_specs=P(("expert", "shard"), "client"),
        check_vma=False,
    )
```

profile of v0, /device:TPU:1, one launch (start us, length us, event | category | flops | bytes accessed | tf_op | source)
XLA Modules:
  0.0 610.1 jit_solution(7069356703528246979)
XLA Ops:
  6.5 2.2 pad_maximum_fusion
  10.4 1.4 scatter_custom_fusion
  11.9 1.4 gather_fusion
  13.5 1.6 broadcast_in_dim.54
  15.1 7.6 %all-to-all-start = ((bf16[16,32,2048]{2,1,0:T(8,128)(2,1)}), bf16[16,32,2048]{2,1,0:T(8,128)(2,1)S(1)}, u32[]{:S(2)}, u32[]{:S(2)}) async-start(bf16[16,32,2048]{2,1,0:T(8,128)(2,1)} %bitcast.7), calls=%async_computation | async-start | bytes 4194304 | tf_op jit(solution)/shard_map/all_to_all | solution.py:71
  23.5 24.8 %all-to-all-done = bf16[16,32,2048]{2,1,0:T(8,128)(2,1)S(1)} async-done(((bf16[16,32,2048]{2,1,0:T(8,128)(2,1)}), bf16[16,32,2048]{2,1,0:T(8,128)(2,1)S(1)}, u32[]{:S(2)}, u32[]{:S(2)}) %all-to-all-start) | async-done | bytes 2097184 | tf_op jit(solution)/shard_map/all_to_all | solution.py:71
  48.3 113.6 %all-gather.5.cloned.1.call-done = bf16[896,2048]{1,0:T(8,128)(2,1)} async-done(((bf16[896,512]{1,0:T(8,128)(2,1)}), bf16[896,2048]{1,0:T(8,128)(2,1)}) %all-gather.5.cloned.1.call-update) | async-done | bytes 3670032 | tf_op jit(solution)/shard_map/all_gather | solution.py:17
  161.9 2.8 fusion.8
  164.7 1.3 fusion.15
  165.9 77.4 %all-gather.7.cloned.1.call-done = bf16[448,2048]{1,0:T(8,128)(2,1)} async-done(((bf16[448,512]{1,0:T(8,128)(2,1)}), bf16[448,2048]{1,0:T(8,128)(2,1)}) %all-gather.7.cloned.1.call-update) | async-done | bytes 1835024 | tf_op jit(solution)/shard_map/all_gather | solution.py:78
  243.4 2.8 multiply_convert_fusion.1
  246.9 1.8 copy.45
  248.7 4.9 all-to-all-start.1
  254.3 47.4 %all-to-all-done.1 = bf16[8,16,32,256]{3,2,1,0:T(8,128)(2,1)S(1)} async-done(((bf16[8,16,32,256]{3,2,1,0:T(8,128)(2,1)}), bf16[8,16,32,256]{3,2,1,0:T(8,128)(2,1)S(1)}, u32[]{:S(2)}, u32[]{:S(2)}) %all-to-all-start.1) | async-done | bytes 2097184 | tf_op jit(solution)/shard_map/all_to_all | solution.py:28
  301.7 1.1 reduce_sum.74
  302.8 7.1 %all-to-all-start.2 = ((bf16[16,32,256]{2,1,0:T(8,128)(2,1)}), bf16[16,32,256]{2,1,0:T(8,128)(2,1)S(1)}, u32[]{:S(2)}, u32[]{:S(2)}) async-start(bf16[16,32,256]{2,1,0:T(8,128)(2,1)} %reduce_sum.74), calls=%async_computation.2 | async-start | bytes 524288 | tf_op jit(solution)/shard_map/all_to_all | solution.py:113
  311.1 6.5 %all-to-all-done.2 = bf16[16,32,256]{2,1,0:T(8,128)(2,1)S(1)} async-done(((bf16[16,32,256]{2,1,0:T(8,128)(2,1)}), bf16[16,32,256]{2,1,0:T(8,128)(2,1)S(1)}, u32[]{:S(2)}, u32[]{:S(2)}) %all-to-all-start.2) | async-done | bytes 262176 | tf_op jit(solution)/shard_map/all_to_all | solution.py:113
  318.0 1.0 gather_fusion.1
  320.9 1.2 gather_fusion.2
  322.2 10.8 %all_to_all.40 = bf16[16,32,256]{2,1,0:T(8,128)(2,1)} all-to-all(bf16[16,32,256]{2,1,0:T(8,128)(2,1)S(1)} %bitcast.81), channel_id=1, replica_groups=mesh['client'=4,'expert'=16,'shard'=8] {'expert'}, dimensions={0} | all-to-all | bytes 524288 | tf_op jit(solution)/shard_map/all_to_all | solution.py:127
  333.3 40.3 %all-gather.9.cloned.1.call-done = bf16[16,32,2048]{2,1,0:T(8,128)(2,1)} async-done(((bf16[16,32,256]{2,1,0:T(8,128)(2,1)}), bf16[16,32,2048]{2,1,0:T(8,128)(2,1)}) %all-gather.9.cloned.1.call-update) | async-done | bytes 2097168 | tf_op jit(solution)/shard_map/all_gather | solution.py:128
  373.5 2.9 fusion.34
  376.4 1.3 multiply_convert_fusion
  379.4 51.2 %all_to_all.41 = bf16[8,16,32,256]{3,2,1,0:T(8,128)(2,1)} all-to-all(bf16[8,16,32,256]{3,2,1,0:T(8,128)(2,1)S(1)} %bitcast.73), channel_id=1, replica_groups=mesh['client'=4,'expert'=16,'shard'=8] {'shard'}, dimensions={0} | all-to-all | bytes 4194304 | tf_op jit(solution)/shard_map/all_to_all | solution.py:28
  430.6 2.0 reduce_sum.76
  432.6 14.0 %all_to_all.42 = bf16[16,32,256]{2,1,0:T(8,128)(2,1)S(1)} all-to-all(bf16[16,32,256]{2,1,0:T(8,128)(2,1)S(1)} %reduce_sum.76), channel_id=1, replica_groups=mesh['client'=4,'expert'=16,'shard'=8] {'expert'}, dimensions={0} | all-to-all | bytes 524288 | tf_op jit(solution)/shard_map/all_to_all | solution.py:113
  449.9 1.2 gather_fusion.4
  451.2 10.8 %all_to_all.43 = bf16[16,32,256]{2,1,0:T(8,128)(2,1)} all-to-all(bf16[16,32,256]{2,1,0:T(8,128)(2,1)S(1)} %bitcast.82), channel_id=1, replica_groups=mesh['client'=4,'expert'=16,'shard'=8] {'expert'}, dimensions={0} | all-to-all | bytes 524288 | tf_op jit(solution)/shard_map/all_to_all | solution.py:127
  464.1 40.1 %all-gather.11.cloned.1.call-done = bf16[16,32,2048]{2,1,0:T(8,128)(2,1)} async-done(((bf16[16,32,256]{2,1,0:T(8,128)(2,1)}), bf16[16,32,2048]{2,1,0:T(8,128)(2,1)}) %all-gather.11.cloned.1.call-update) | async-done | bytes 2097168 | tf_op jit(solution)/shard_map/all_gather | solution.py:128
  504.2 4.0 fusion.4
  508.4 94.0 %all_to_all.44 = bf16[448,4,512]{2,0,1:T(8,128)(2,1)S(1)} all-to-all(bf16[448,4,512]{2,0,1:T(8,128)(2,1)S(1)} %bitcast.74), channel_id=1, replica_groups=mesh['client'=4,'expert'=16,'shard'=8] {'client'}, dimensions={1} | all-to-all | bytes 3670016 | tf_op jit(solution)/shard_map/all_to_all | solution.py:141
  602.4 1.2 convert_reduce_fusion
  (80 shorter events, 13.5 us)
Async XLA Ops:
  6.5 5.4 copy-start
  6.5 2.2 copy-start.5
  6.5 155.3 %all-gather.5.cloned.1.call-start = ((), (), s32[]{:S(2)}) async-start(), calls=%async_computation.8 | async-start | bytes 4587520 | tf_op jit(solution)/shard_map/all_gather | solution.py:17
  15.1 33.2 %all-to-all-start = ((bf16[16,32,2048]{2,1,0:T(8,128)(2,1)}), bf16[16,32,2048]{2,1,0:T(8,128)(2,1)S(1)}, u32[]{:S(2)}, u32[]{:S(2)}) async-start(bf16[16,32,2048]{2,1,0:T(8,128)(2,1)} %bitcast.7), calls=%async_computation | async-start | bytes 4194304 | tf_op jit(solution)/shard_map/all_to_all | solution.py:71
  22.7 220.7 %all-gather.7.cloned.1.call-start = ((), (), s32[]{:S(2)}) async-start(), calls=%async_computation.9 | async-start | bytes 2293760 | tf_op jit(solution)/shard_map/all_gather | solution.py:78
  161.9 2.8 copy-start.6
  248.7 4.9 copy-start.7
  248.7 53.0 %all-to-all-start.1 = ((bf16[8,16,32,256]{3,2,1,0:T(8,128)(2,1)}), bf16[8,16,32,256]{3,2,1,0:T(8,128)(2,1)S(1)}, u32[]{:S(2)}, u32[]{:S(2)}) async-start(bf16[8,16,32,256]{3,2,1,0:T(8,128)(2,1)} %bitcast.70), calls=%async_computation.1 | async-start | bytes 4194304 | tf_op jit(solution)/shard_map/all_to_all | solution.py:28
  253.6 57.1 %copy-start.4 = (f32[1,128,2]{1,2,0:T(2,128)S(1)}, f32[1,128,2]{1,2,0:T(2,128)}, u32[]{:S(2)}) copy-start(f32[1,128,2]{1,2,0:T(2,128)} %param.16) | copy-start | bytes 3076
  302.8 14.8 %all-to-all-start.2 = ((bf16[16,32,256]{2,1,0:T(8,128)(2,1)}), bf16[16,32,256]{2,1,0:T(8,128)(2,1)S(1)}, u32[]{:S(2)}, u32[]{:S(2)}) async-start(bf16[16,32,256]{2,1,0:T(8,128)(2,1)} %reduce_sum.74), calls=%async_computation.2 | async-start | bytes 524288 | tf_op jit(solution)/shard_map/all_to_all | solution.py:113
  309.9 63.6 %all-gather.9.cloned.1.call-start = ((), (), s32[]{:S(2)}) async-start(), calls=%async_computation.10 | async-start | bytes 2359296 | tf_op jit(solution)/shard_map/all_gather | solution.py:128
  333.1 171.1 %all-gather.11.cloned.1.call-start = ((), (), s32[]{:S(2)}) async-start(), calls=%async_computation.11 | async-start | bytes 2359296 | tf_op jit(solution)/shard_map/all_gather | solution.py:128
  373.5 2.9 copy-start.2
  373.5 2.9 copy-start.3
  376.4 1.8 copy-start.1
Sparse Core Ops, SparseCore 0:
  9.4 152.4 all-gather.4
  164.0 79.3 all-gather.6
  333.2 40.3 all-gather.8
  462.2 41.9 all-gather.10
where the time goes:
time: 611 us; the launch traced here: 610 us
  waiting for transfers between devices  351 us (57%)
  blocking collectives  181 us (30%)
  starting transfers between devices  19.9 us (3%)
  local copies, waits for them, and re-layouts  15.9 us (3%)
  matrix products  15.6 us (3%)
  between operations  15 us (2%)
  other arithmetic  12 us (2%)
    all_gather x1, waiting for transfers between devices, sent_together(): lax.all_gather(both, axis, axis=dim, tiled=True)  114 us
    all_to_all x1, blocking collectives, local(): lax.all_to_all(client_term, 'client', split_axis=1, concat_axis=1, tiled=...  94 us
    all_gather x2, waiting for transfers between devices, local(): arrived = own_of(lax.all_gather(arrived, 'shard', axis=2, tiled=True))  80.4 us
    all_gather x1, waiting for transfers between devices, local(): down_full = lax.all_gather(down_proj, 'client', axis=1, tiled=True)  77.4 us
    all_to_all x1, blocking collectives, sum_at_owner(): parts = lax.all_to_all(in_blocks(x, dim, peers), axis, 0, 0, tiled=True)  51.2 us
    all_to_all x1, waiting for transfers between devices, sum_at_owner(): parts = lax.all_to_all(in_blocks(x, dim, peers), axis, 0, 0, tiled=True)  47.4 us
    all_to_all x1, waiting for transfers between devices, local(): lax.all_to_all(send_blocks, 'expert', split_axis=0, concat_axis=0, tiled=...  24.8 us
    all_to_all x2, blocking collectives, local(): lax.all_to_all(blocks, 'expert', split_axis=0, concat_axis=0, tiled=True)  21.6 us
  transfers between devices with their start and end apart: 7, of which 7 were waited for; matrix products, arithmetic and copies ran while one was open for 2% of the time, Pallas kernels for 0%

commit v1 on v0

--- a/solution.py
+++ b/solution.py
@@ -125,7 +125,11 @@
         cotangent = cotangent.reshape(token_count * top_count, share_width)
         blocks = arrange(jnp.take(cotangent, source_of, axis=0), share_width)
         arrived = lax.all_to_all(blocks, "expert", split_axis=0, concat_axis=0, tiled=True)
-        arrived = own_of(lax.all_gather(arrived, "shard", axis=2, tiled=True))
+        arrived = own_of(
+            jnp.concatenate(
+                lax.all_to_all(jnp.stack([arrived] * lax.axis_size("shard")), "shard", 0, 0), axis=2
+            )
+        )
         gradient = lax.dot_general(
             hidden, arrived, (((0,), (0,)), ((), ())), preferred_element_type=jnp.float32
         )

time: 611 us -> 640 us (1.047)
  blocking collectives: 181 us -> 228 us
  waiting for transfers between devices: 351 us -> 317 us
  local copies, waits for them, and re-layouts: 15.9 us -> 25.8 us
  starting transfers between devices: 19.9 us -> 27.5 us
    all_gather x2 -> x0, waiting for transfers between devices: 80.4 us -> none  [local(): arrived = own_of(lax.all_gather(arrived, 'shard', axis=2, tiled=True))]
    all_to_all x0 -> x1, blocking collectives: none -> 54.1 us  [local(): lax.all_to_all(jnp.stack([arrived] * lax.axis_size('shard')), 'shard', 0, 0)]
    all_to_all x0 -> x1, waiting for transfers between devices: none -> 46.3 us  [local(): lax.all_to_all(jnp.stack([arrived] * lax.axis_size('shard')), 'shard', 0, 0)]
    all_to_all x0 -> x1, starting transfers between devices: none -> 7.82 us  [local(): lax.all_to_all(jnp.stack([arrived] * lax.axis_size('shard')), 'shard', 0, 0)]
  transfers between devices with their start and end apart: 7 -> 6, of which waited for: 7 -> 6; matrix products, arithmetic and copies ran while one was open for 2% -> 2% of each run, Pallas kernels for 0% -> 0%
where the time goes in v1:
time: 640 us; the launch traced here: 637 us
  waiting for transfers between devices  317 us (50%)
  blocking collectives  228 us (36%)
  starting transfers between devices  27.5 us (4%)
  local copies, waits for them, and re-layouts  25.8 us (4%)
  between operations  15.2 us (2%)
  other arithmetic  11.9 us (2%)
  matrix products  11.3 us (2%)
    all_gather x1, waiting for transfers between devices, sent_together(): lax.all_gather(both, axis, axis=dim, tiled=True)  114 us
    all_to_all x1, blocking collectives, local(): lax.all_to_all(client_term, 'client', split_axis=1, concat_axis=1, tiled=...  91.1 us
    all_gather x1, waiting for transfers between devices, local(): down_full = lax.all_gather(down_proj, 'client', axis=1, tiled=True)  77.4 us
    all_to_all x1, blocking collectives, local(): lax.all_to_all(jnp.stack([arrived] * lax.axis_size('shard')), 'shard', 0, 0)  54.1 us
    all_to_all x1, blocking collectives, sum_at_owner(): parts = lax.all_to_all(in_blocks(x, dim, peers), axis, 0, 0, tiled=True)  52.2 us
    all_to_all x1, waiting for transfers between devices, sum_at_owner(): parts = lax.all_to_all(in_blocks(x, dim, peers), axis, 0, 0, tiled=True)  47.4 us
    all_to_all x1, waiting for transfers between devices, local(): lax.all_to_all(jnp.stack([arrived] * lax.axis_size('shard')), 'shard', 0, 0)  46.3 us
    all_to_all x1, waiting for transfers between devices, local(): lax.all_to_all(send_blocks, 'expert', split_axis=0, concat_axis=0, tiled=...  24.8 us
  transfers between devices with their start and end apart: 6, of which 6 were waited for; matrix products, arithmetic and copies ran while one was open for 2% of the time, Pallas kernels for 0%

profile of v1, /device:TPU:1, one launch (start us, length us, event | category | flops | bytes accessed | tf_op | source)
XLA Modules:
  0.0 636.8 jit_solution(3160299699553065373)
XLA Ops:
  6.5 2.2 pad_maximum_fusion
  10.4 1.4 scatter_custom_fusion
  11.9 1.4 gather_fusion
  13.5 1.6 broadcast_in_dim.54
  15.1 7.6 %all-to-all-start = ((bf16[16,32,2048]{2,1,0:T(8,128)(2,1)}), bf16[16,32,2048]{2,1,0:T(8,128)(2,1)S(1)}, u32[]{:S(2)}, u32[]{:S(2)}) async-start(bf16[16,32,2048]{2,1,0:T(8,128)(2,1)} %bitcast.7), calls=%async_computation | async-start | bytes 4194304 | tf_op jit(solution)/shard_map/all_to_all | solution.py:71
  23.5 24.8 %all-to-all-done = bf16[16,32,2048]{2,1,0:T(8,128)(2,1)S(1)} async-done(((bf16[16,32,2048]{2,1,0:T(8,128)(2,1)}), bf16[16,32,2048]{2,1,0:T(8,128)(2,1)S(1)}, u32[]{:S(2)}, u32[]{:S(2)}) %all-to-all-start) | async-done | bytes 2097184 | tf_op jit(solution)/shard_map/all_to_all | solution.py:71
  48.3 113.6 %all-gather.3.cloned.1.call-done = bf16[896,2048]{1,0:T(8,128)(2,1)} async-done(((bf16[896,512]{1,0:T(8,128)(2,1)}), bf16[896,2048]{1,0:T(8,128)(2,1)}) %all-gather.3.cloned.1.call-update) | async-done | bytes 3670032 | tf_op jit(solution)/shard_map/all_gather | solution.py:17
  161.9 2.8 fusion.8
  164.7 1.3 fusion.15
  165.9 77.4 %all-gather.5.cloned.1.call-done = bf16[448,2048]{1,0:T(8,128)(2,1)} async-done(((bf16[448,512]{1,0:T(8,128)(2,1)}), bf16[448,2048]{1,0:T(8,128)(2,1)}) %all-gather.5.cloned.1.call-update) | async-done | bytes 1835024 | tf_op jit(solution)/shard_map/all_gather | solution.py:78
  243.4 2.8 multiply_convert_fusion.1
  246.9 1.8 copy.49
  248.7 4.9 all-to-all-start.1
  254.3 47.4 %all-to-all-done.1 = bf16[8,16,32,256]{3,2,1,0:T(8,128)(2,1)S(1)} async-done(((bf16[8,16,32,256]{3,2,1,0:T(8,128)(2,1)}), bf16[8,16,32,256]{3,2,1,0:T(8,128)(2,1)S(1)}, u32[]{:S(2)}, u32[]{:S(2)}) %all-to-all-start.1) | async-done | bytes 2097184 | tf_op jit(solution)/shard_map/all_to_all | solution.py:28
  302.8 7.1 %all-to-all-start.2 = ((bf16[16,32,256]{2,1,0:T(8,128)(2,1)}), bf16[16,32,256]{2,1,0:T(8,128)(2,1)S(1)}, u32[]{:S(2)}, u32[]{:S(2)}) async-start(bf16[16,32,256]{2,1,0:T(8,128)(2,1)} %reduce_sum.74), calls=%async_computation.2 | async-start | bytes 524288 | tf_op jit(solution)/shard_map/all_to_all | solution.py:113
  311.0 6.7 %all-to-all-done.2 = bf16[16,32,256]{2,1,0:T(8,128)(2,1)S(1)} async-done(((bf16[16,32,256]{2,1,0:T(8,128)(2,1)}), bf16[16,32,256]{2,1,0:T(8,128)(2,1)S(1)}, u32[]{:S(2)}, u32[]{:S(2)}) %all-to-all-start.2) | async-done | bytes 262176 | tf_op jit(solution)/shard_map/all_to_all | solution.py:113
  322.2 10.3 %all_to_all.50 = bf16[16,32,256]{2,1,0:T(8,128)(2,1)S(1)} all-to-all(bf16[16,32,256]{2,1,0:T(8,128)(2,1)S(1)} %bitcast.90), channel_id=1, replica_groups=mesh['client'=4,'expert'=16,'shard'=8] {'expert'}, dimensions={0} | all-to-all | bytes 524288 | tf_op jit(solution)/shard_map/all_to_all | solution.py:127
  332.8 54.1 %all_to_all.51 = bf16[8,16,32,256]{3,2,1,0:T(8,128)(2,1)S(1)} all-to-all(bf16[8,16,32,256]{3,2,1,0:T(8,128)(2,1)S(1)} %stack.4), channel_id=1, replica_groups=mesh['client'=4,'expert'=16,'shard'=8] {'shard'}, dimensions={0} | all-to-all | bytes 4194304 | tf_op jit(solution)/shard_map/all_to_all | solution.py:130
  386.9 1.4 copy.27
  391.1 1.3 multiply_convert_fusion
  394.0 52.2 %all_to_all.52 = bf16[8,16,32,256]{3,2,1,0:T(8,128)(2,1)} all-to-all(bf16[8,16,32,256]{3,2,1,0:T(8,128)(2,1)S(1)} %bitcast.83), channel_id=1, replica_groups=mesh['client'=4,'expert'=16,'shard'=8] {'shard'}, dimensions={0} | all-to-all | bytes 4194304 | tf_op jit(solution)/shard_map/all_to_all | solution.py:28
  446.2 2.0 reduce_sum.76
  448.2 10.3 %all_to_all.53 = bf16[16,32,256]{2,1,0:T(8,128)(2,1)S(1)} all-to-all(bf16[16,32,256]{2,1,0:T(8,128)(2,1)S(1)} %reduce_sum.76), channel_id=1, replica_groups=mesh['client'=4,'expert'=16,'shard'=8] {'expert'}, dimensions={0} | all-to-all | bytes 524288 | tf_op jit(solution)/shard_map/all_to_all | solution.py:113
  463.1 10.3 %all_to_all.54 = bf16[16,32,256]{2,1,0:T(8,128)(2,1)S(1)} all-to-all(bf16[16,32,256]{2,1,0:T(8,128)(2,1)S(1)} %bitcast.91), channel_id=1, replica_groups=mesh['client'=4,'expert'=16,'shard'=8] {'expert'}, dimensions={0} | all-to-all | bytes 524288 | tf_op jit(solution)/shard_map/all_to_all | solution.py:127
  473.4 1.6 stack.5
  475.0 7.8 %all-to-all-start.8 = ((bf16[8,16,32,256]{3,2,1,0:T(8,128)(2,1)}), bf16[8,16,32,256]{3,2,1,0:T(8,128)(2,1)}, u32[]{:S(2)}, u32[]{:S(2)}) async-start(bf16[8,16,32,256]{3,2,1,0:T(8,128)(2,1)} %stack.5), calls=%async_computation.8 | async-start | bytes 4194304 | tf_op jit(solution)/shard_map/all_to_all | solution.py:130
  484.8 46.3 %all-to-all-done.8 = bf16[8,16,32,256]{3,2,1,0:T(8,128)(2,1)} async-done(((bf16[8,16,32,256]{3,2,1,0:T(8,128)(2,1)}), bf16[8,16,32,256]{3,2,1,0:T(8,128)(2,1)}, u32[]{:S(2)}, u32[]{:S(2)}) %all-to-all-start.8) | async-done | bytes 2097184 | tf_op jit(solution)/shard_map/all_to_all | solution.py:130
  531.0 3.0 copy.32
  534.7 1.3 copy-done.3
  536.1 1.5 fusion.4
  537.7 91.1 %all_to_all.55 = bf16[448,4,512]{2,0,1:T(8,128)(2,1)S(1)} all-to-all(bf16[448,4,512]{2,0,1:T(8,128)(2,1)S(1)} %bitcast.85), channel_id=1, replica_groups=mesh['client'=4,'expert'=16,'shard'=8] {'client'}, dimensions={1} | all-to-all | bytes 3670016 | tf_op jit(solution)/shard_map/all_to_all | solution.py:145
  628.8 1.2 convert_reduce_fusion
  (87 shorter events, 21.2 us)
Async XLA Ops:
  6.5 5.4 copy-start
  6.5 2.2 copy-start.7
  6.5 155.3 %all-gather.3.cloned.1.call-start = ((), (), s32[]{:S(2)}) async-start(), calls=%async_computation.10 | async-start | bytes 4587520 | tf_op jit(solution)/shard_map/all_gather | solution.py:17
  15.1 33.2 %all-to-all-start = ((bf16[16,32,2048]{2,1,0:T(8,128)(2,1)}), bf16[16,32,2048]{2,1,0:T(8,128)(2,1)S(1)}, u32[]{:S(2)}, u32[]{:S(2)}) async-start(bf16[16,32,2048]{2,1,0:T(8,128)(2,1)} %bitcast.7), calls=%async_computation | async-start | bytes 4194304 | tf_op jit(solution)/shard_map/all_to_all | solution.py:71
  22.7 220.7 %all-gather.5.cloned.1.call-start = ((), (), s32[]{:S(2)}) async-start(), calls=%async_computation.11 | async-start | bytes 2293760 | tf_op jit(solution)/shard_map/all_gather | solution.py:78
  161.9 2.8 copy-start.8
  248.7 4.9 copy-start.9
  248.7 53.0 %all-to-all-start.1 = ((bf16[8,16,32,256]{3,2,1,0:T(8,128)(2,1)}), bf16[8,16,32,256]{3,2,1,0:T(8,128)(2,1)S(1)}, u32[]{:S(2)}, u32[]{:S(2)}) async-start(bf16[8,16,32,256]{3,2,1,0:T(8,128)(2,1)} %bitcast.77), calls=%async_computation.1 | async-start | bytes 4194304 | tf_op jit(solution)/shard_map/all_to_all | solution.py:28
  253.6 57.0 %copy-start.6 = (f32[1,128,2]{1,2,0:T(2,128)S(1)}, f32[1,128,2]{1,2,0:T(2,128)}, u32[]{:S(2)}) copy-start(f32[1,128,2]{1,2,0:T(2,128)} %param.16) | copy-start | bytes 3076
  302.8 14.8 %all-to-all-start.2 = ((bf16[16,32,256]{2,1,0:T(8,128)(2,1)}), bf16[16,32,256]{2,1,0:T(8,128)(2,1)S(1)}, u32[]{:S(2)}, u32[]{:S(2)}) async-start(bf16[16,32,256]{2,1,0:T(8,128)(2,1)} %reduce_sum.74), calls=%async_computation.2 | async-start | bytes 524288 | tf_op jit(solution)/shard_map/all_to_all | solution.py:113
  389.0 1.5 copy-start.4
  389.0 2.0 copy-start.5
  391.1 1.8 copy-start.2
  475.0 56.0 %all-to-all-start.8 = ((bf16[8,16,32,256]{3,2,1,0:T(8,128)(2,1)}), bf16[8,16,32,256]{3,2,1,0:T(8,128)(2,1)}, u32[]{:S(2)}, u32[]{:S(2)}) async-start(bf16[8,16,32,256]{3,2,1,0:T(8,128)(2,1)} %stack.5), calls=%async_computation.8 | async-start | bytes 4194304 | tf_op jit(solution)/shard_map/all_to_all | solution.py:130
  534.0 2.0 copy-start.3
  537.7 92.3 %copy-start.1 = (bf16[1,128,2048]{2,1,0:T(8,128)(2,1)S(1)}, bf16[1,128,2048]{2,1,0:T(8,128)(2,1)}, u32[]{:S(2)}) copy-start(bf16[1,128,2048]{2,1,0:T(8,128)(2,1)} %param.13) | copy-start | bytes 1572868
Sparse Core Ops, SparseCore 0:
  9.4 152.4 all-gather.2
  164.0 79.3 all-gather.4
